TPU v7x, 32 devices: a whole 2x2x4 slice. The times are simulated.
32 devices in a mesh: lon: 4 (over z), lat: 4 (over x, core), mem: 2 (over y).
Axes of the slice: x: 2, y: 2, z: 4, core: 2. Of those that a mesh axis runs over, the one named last changes fastest.
Arguments:
- tokens: bfloat16 [4, 8, 136, 24, 192], P('mem', None, 'lat', 'lon'), parts along dimension 0, may hold values from -6 to 6
- band_rows: int32 [4, 2], P('lat'), may hold values from 0 to 89, as said below
- down_gain: float32 [768], replicated, may hold values from 0.1 to 1.9
- down_shift: float32 [768], replicated, may hold values from -3 to 3
- down_weight: bfloat16 [768, 384], P(('lon', 'lat')), may hold values from -0.21875 to 0.21875
- up_weight: bfloat16 [384, 768], P(('lon', 'lat')), may hold values from -0.3125 to 0.3125
- up_gain: float32 [192], replicated, may hold values from 0.1 to 1.9
- up_shift: float32 [192], replicated, may hold values from -3 to 3
- mix_weight: bfloat16 [192, 192], replicated, may hold values from -0.4375 to 0.4375
Outputs:
- expanded: bfloat16 [4, 8, 136, 24, 192], P('mem', None, 'lat', 'lon'), parts along dimension 0
There are 2 independent parts, one for each index of `mem`. A program takes and returns all parts, laid end to end along the dimension named above; an argument that names none is the same for every part. Nothing has to cross between parts.
Inputs may be any that keep to these rules, and one draw needn't show every extreme that they name: `band_rows`: row b holds band b's first latitude row and one past its last; the bands cover rows 0 to 88 in order without gaps; band 0 holds an odd number of rows and every other band an even number; each band holds at least 2 * (5) rows and at most 34, and some band other than band 0 holds exactly 34.
All inputs are finite; a program needn't handle non-finite values.
Results may differ from a plain program's by a relative error of at most 0.0062.
Values may be sent and summed in bfloat16 or wider, within the bound.
A program may use at most 64 MiB of HBM per device.

v0:
```python
import jax
import jax.numpy as jnp
from jax import lax
from jax.sharding import PartitionSpec as P


def shifted(block, axis, distance):
    devices = range(lax.axis_size(axis))
    route = [((i - distance) % len(devices), i) for i in devices]
    return lax.ppermute(block, axis, route)


def passed_along(block, axis, distance):
    devices = range(lax.axis_size(axis))
    route = [(i - distance, i) for i in devices if i - distance in devices]
    return lax.ppermute(block, axis, route)


def normalize(values, scale_gain, bias_shift):
    average = jnp.mean(values, axis=-1, keepdims=True)
    centred = values - average
    spread = jnp.mean(centred * centred, axis=-1, keepdims=True)
    return centred * lax.rsqrt(spread + 1e-05) * scale_gain + bias_shift


def body(
    tokens, band_rows, down_gain, down_shift, down_weight, up_weight, up_gain, up_shift, mix_weight
):
    members, levels, slot_count, columns, features = tokens.shape
    half_rows = slot_count // 2 + 1
    first_row = band_rows[0, 0]
    live_rows = band_rows[0, 1] - first_row
    lat_odd = first_row % 2
    row_ids = lax.broadcasted_iota(jnp.int32, (1, 1, slot_count, 1, 1), 2)
    fields = jnp.where(row_ids < live_rows, tokens, jnp.zeros_like(tokens))
    right_col = shifted(fields[:, :, :, :1], "lon", -1)
    window = jnp.concatenate([fields[:, :, :, 1:], right_col], axis=3)
    window_cols = window.shape[3]
    half_cols = window_cols // 2
    next_first = passed_along(window[:, :, :1], "lat", -1)
    zero_rows = jnp.zeros((members, levels, 2, window_cols, features), window.dtype)
    extended = jnp.concatenate([window, zero_rows, zero_rows[:, :, :1]], axis=2)
    ext_ids = lax.broadcasted_iota(jnp.int32, (1, 1, slot_count + 3, 1, 1), 2)
    extended = jnp.where(ext_ids == live_rows, next_first, extended)
    patch_rows = lax.dynamic_slice_in_dim(extended, lat_odd, 2 * half_rows, 2)
    merged = patch_rows.reshape(members, levels, half_rows, 2, half_cols, 2, features)
    merged = merged.transpose(0, 1, 2, 4, 5, 3, 6).reshape(
        members * levels * half_rows * half_cols, 4 * features
    )
    merged_norm = normalize(merged.astype(jnp.float32), down_gain, down_shift).astype(jnp.bfloat16)
    columns_used = merged_norm
    coarse = jnp.dot(
        columns_used,
        lax.all_gather(down_weight, ("lon", "lat"), axis=0, tiled=True),
        preferred_element_type=jnp.float32,
    )
    coarse = coarse.astype(jnp.bfloat16)
    columns_used = coarse
    grown = jnp.dot(
        columns_used,
        lax.all_gather(up_weight, ("lon", "lat"), axis=0, tiled=True),
        preferred_element_type=jnp.float32,
    )
    grown = grown.reshape(members, levels, half_rows, half_cols, 2, 2, features)
    grown = grown.transpose(0, 1, 2, 4, 3, 5, 6).reshape(
        members, levels, 2 * half_rows, window_cols, features
    )
    fine_norm = normalize(grown, up_gain, up_shift).astype(jnp.bfloat16)
    fine_out = jnp.dot(
        fine_norm.reshape(-1, features), mix_weight, preferred_element_type=jnp.float32
    )
    fine_out = fine_out.astype(jnp.bfloat16).reshape(
        members, levels, 2 * half_rows, window_cols, features
    )
    overflow_row = lax.dynamic_slice_in_dim(fine_out, live_rows - lat_odd, 1, 2)
    from_above = passed_along(overflow_row, "lat", 1)
    padded_rows = jnp.concatenate([jnp.zeros_like(overflow_row), fine_out], axis=2)
    owned = lax.dynamic_slice_in_dim(padded_rows, 1 - lat_odd, slot_count, 2)
    owned = jnp.where((row_ids == 0) & (lat_odd == 1), from_above, owned)
    overflow_col = owned[:, :, :, columns - 1 :]
    from_left = shifted(overflow_col, "lon", 1)
    owned = jnp.concatenate([from_left, owned[:, :, :, : columns - 1]], axis=3)
    return jnp.where(row_ids < live_rows, owned, jnp.zeros_like(owned))


def solution(mesh):
    return jax.shard_map(
        body,
        mesh=mesh,
        in_specs=(
            P("mem", None, "lat", "lon", None),
            P("lat", None),
            P(),
            P(),
            P(("lon", "lat"), None),
            P(("lon", "lat"), None),
            P(),
            P(),
            P(),
        ),
        out_specs=P("mem", None, "lat", "lon", None),
        check_vma=False,
    )
```

profile of v0, /device:TPU:0, one launch (start us, length us, event | category | flops | bytes accessed | tf_op | source)
XLA Modules:
  0.0 134.9 jit_solution(14760807719825916473)
XLA Ops:
  0.0 1.3 fusion.16
  2.6 1.6 %broadcast_select_fusion = bf16[2,8,34,6,192]{4,1,3,2,0:T(8,128)(2,1)S(1)} fusion(bf16[2,8,34,6,192]{4,1,3,2,0:T(8,128)(2,1)} %param.9, pred[34]{0:T(512)(128)(4,1)S(1)} %iota_compare_fusion.1), kind=kLoop, calls=%fused_computation.21 | loop fusion | flops 626688 | bytes 2506786 | tf_op jit(solution)/shard_map/jit(_where)/select_n | solution.py:35
  4.2 0.7 slice.29
  5.0 5.1 %collective-permute-start = (bf16[2,8,34,1,192]{4,1,3,2,0:T(8,128)(2,1)}, bf16[2,8,34,1,192]{4,1,3,2,0:T(8,128)(2,1)S(1)}, u32[]{:S(2)}, u32[]{:S(2)}) collective-permute-start(bf16[2,8,34,1,192]{4,1,3,2,0:T(8,128)(2,1)} %slice.29), channel_id=1, source_target_pairs={{8,0},{16,8},{24,16},{0,24},{9,1},{17,9},{25,17},{1,25},{10,2},{18... | collective-permute-start | bytes 626696 | tf_op jit(solution)/shard_map/ppermute | solution.py:10
  12.0 22.9 %all_gather.6 = bf16[768,384]{1,0:T(8,128)(2,1)} all-gather(bf16[48,384]{1,0:T(8,128)(2,1)S(1)} %copy-done.4), channel_id=1, replica_groups=mesh['lon'=4,'lat'=4,'mem'=2] {'lon','lat'}, dimensions={0}, use_global_device_ids=true | all-gather | bytes 626688 | tf_op jit(solution)/shard_map/all_gather | solution.py:54
  35.0 20.4 %all_gather.7 = bf16[384,768]{1,0:T(8,128)(2,1)} all-gather(bf16[24,768]{1,0:T(8,128)(2,1)S(1)} %copy-done.5), channel_id=1, replica_groups=mesh['lon'=4,'lat'=4,'mem'=2] {'lon','lat'}, dimensions={0}, use_global_device_ids=true | all-gather | bytes 626688 | tf_op jit(solution)/shard_map/all_gather | solution.py:61
  55.4 1.3 collective-permute-start.1
  57.0 1.5 %collective-permute-done.1 = bf16[2,8,1,6,192]{4,1,3,2,0:T(8,128)(2,1)S(1)} collective-permute-done((bf16[2,8,1,6,192]{4,1,3,2,0:T(8,128)(2,1)S(1)}, bf16[2,8,1,6,192]{4,1,3,2,0:T(8,128)(2,1)S(1)}, u32[]{:S(2)}, u32[]{:S(2)}) %collective-permute-start.1) | collective-permute-done | bytes 36896 | tf_op jit(solution)/shard_map/ppermute | solution.py:16
  58.5 0.6 copy-done.3
  59.2 1.4 %fusion.3 = bf16[2,8,36,6,192]{4,1,3,2,0:T(8,128)(2,1)S(1)} fusion(s32[]{:T(128)S(6)} %select_n.34, bf16[2,8,34,5,192]{4,1,3,2,0:T(8,128)(2,1)S(1)} %slice.28, bf16[2,8,34,1,192]{4,1,3,2,0:T(8,128)(2,1)S(1)} %collective-permute-done, pred[36]{0:T(512)(128)(4,1)S(1)} %dynamic-slice.2, bf16[2,8,6,192]{3,1,2,0:T(8,128)(2,1)} %bitcast.30, ...), kind=kLoop, calls=%fused_computation.13 | loop fusion | flops 2654208 | bytes 2617528 | tf_op jit(solution)/shard_map/jit(_where)/select_n | solution.py:44
  60.6 0.4 fusion.4
  61.4 2.3 %convert_bitcast_fusion = f32[2,8,18,3,2,2,192]{6,1,4,3,5,2,0:T(8,128)} fusion(bf16[2,8,18,2,3,2,192]{6,1,5,4,3,2,0:T(8,128)(2,1)S(1)} %bitcast.26), kind=kLoop, calls=%fused_computation.1 | loop fusion | flops 663552 | bytes 3981312 | tf_op jit(solution)/shard_map/convert_element_type | solution.py:50
  63.7 0.7 multiply_reduce_fusion.1
  65.1 6.5 %copy.32 = f32[2,8,18,3,2,2,192]{6,5,4,3,2,1,0:T(2,128)} copy(f32[2,8,18,3,2,2,192]{6,1,4,3,5,2,0:T(8,128)} %convert_bitcast_fusion) | data formatting | bytes 5308416 | tf_op jit(solution)/shard_map/convert_element_type | solution.py:50
  71.7 4.8 %reshape.108 = f32[864,768]{1,0:T(8,128)S(1)} reshape(f32[2,8,18,3,2,2,192]{6,5,4,3,2,1,0:T(2,128)} %copy.32) | data formatting | bytes 5308416 | tf_op jit(solution)/shard_map/convert_element_type | solution.py:50
  76.5 4.4 %fusion.14 = f32[864,768]{1,0:T(8,128)} fusion(bf16[384,768]{1,0:T(8,128)(2,1)} %all_gather.7, bf16[768,384]{1,0:T(8,128)(2,1)S(1)} %copy-done.2, f32[864,768]{1,0:T(8,128)S(1)} %reshape.108, f32[768]{0:T(1024)S(1)} %copy-done.8, f32[768]{0:T(1024)S(1)} %copy-done.9, f32[864]{0:T(1024)S(1)} %rsqrt.23, f32[864]{0:T(1024)S(1)} %div.17), kind=kOutput, calls=%fused_computation.27 | convolution fusion | flops 1022865408 | bytes 6501120 | tf_op jit(solution)/shard_map/dot_general | solution.py:59
  80.9 6.3 %reshape.105 = f32[2,8,18,3,2,2,192]{6,5,4,3,2,1,0:T(2,128)} reshape(f32[864,768]{1,0:T(8,128)} %fusion.14) | data formatting | bytes 5308416 | tf_op jit(solution)/shard_map/reshape | solution.py:64
  87.2 4.2 %fusion.15 = f32[2,8,18,2,3,2]{5,4,3,2,1,0:T(4,128)S(1)} fusion(f32[2,8,18,3,2,2,192]{6,5,4,3,2,1,0:T(2,128)} %reshape.105), kind=kLoop, calls=%fused_computation.39 | loop fusion | flops 660096 | bytes 2668032 | tf_op jit(solution)/shard_map/reduce_sum | solution.py:20
  91.8 0.6 div.20
  92.4 5.9 %multiply_reduce_fusion = f32[2,8,18,2,3,2]{5,4,3,2,1,0:T(4,128)S(1)} fusion(f32[2,8,18,2,3,2]{5,4,3,2,1,0:T(4,128)S(1)} %broadcast_multiply_fusion, f32[2,8,18,3,2,2,192]{6,5,4,3,2,1,0:T(2,128)} %reshape.105), kind=kLoop, calls=%fused_computation.4 | loop fusion | flops 1987200 | bytes 2681856 | tf_op jit(solution)/shard_map/reduce_sum | solution.py:22
  98.3 3.0 %copy.48 = f32[2,8,18,3,2,2,192]{6,5,3,4,2,1,0:T(2,128)} copy(f32[2,8,18,3,2,2,192]{6,5,4,3,2,1,0:T(2,128)S(1)} %copy-done.1) | data formatting | bytes 5308416 | tf_op jit(solution)/shard_map/reshape | solution.py:64
  101.3 5.4 %reshape.106 = f32[3456,192]{1,0:T(8,128)} reshape(f32[2,8,18,2,3,2,192]{6,5,4,3,2,1,0:T(2,128)} %bitcast.28) | data formatting | bytes 5308416 | tf_op jit(solution)/shard_map/reshape | solution.py:65
  106.7 0.4 add_rsqrt_fusion
  107.1 0.6 rsqrt.25
  107.7 3.3 %convolution_convert_fusion = bf16[3456,192]{0,1:T(8,128)(2,1)S(1)} fusion(bf16[192,192]{1,0:T(8,128)(2,1)S(1)} %copy-done, f32[3456,192]{1,0:T(8,128)} %reshape.106, f32[192]{0:T(256)S(1)} %copy-done.6, f32[192]{0:T(256)S(1)} %copy-done.7, f32[3456]{0:T(1024)S(1)} %rsqrt.25, f32[3456]{0:T(1024)S(1)} %div.20), kind=kOutput, calls=%fused_computation | convolution fusion | flops 258785280 | bytes 4084224 | tf_op jit(solution)/shard_map/dot_general | solution.py:69
  111.0 2.2 %copy.39 = bf16[3456,192]{1,0:T(8,128)(2,1)} copy(bf16[3456,192]{0,1:T(8,128)(2,1)S(1)} %convolution_convert_fusion) | data formatting | bytes 2654208 | tf_op jit(solution)/shard_map/convert_element_type | solution.py:72
  113.2 2.8 %reshape.107 = bf16[2,8,36,6,192]{4,3,2,1,0:T(8,128)(2,1)S(1)} reshape(bf16[3456,192]{1,0:T(8,128)(2,1)} %copy.39) | data formatting | bytes 2654208 | tf_op jit(solution)/shard_map/reshape | solution.py:72
  116.1 4.5 %collective-permute-start.2 = (bf16[2,8,1,6,192]{4,3,2,1,0:T(8,128)(2,1)S(1)}, bf16[2,8,1,6,192]{4,3,2,1,0:T(8,128)(2,1)S(1)}, u32[]{:S(2)}, u32[]{:S(2)}) collective-permute-start(bf16[2,8,1,6,192]{4,3,2,1,0:T(8,128)(2,1)S(1)} %constant_dynamic-slice_fusion), channel_id=1, source_target_pairs={{0,2},{2,4},{4,6},{1,3},{3,5},{5,7},{8,10},{10,12},{12,14},{9,11},... | collective-permute-start | bytes 110600 | tf_op jit(solution)/shard_map/ppermute | solution.py:16
  120.6 1.9 %copy.41 = bf16[2,8,36,6,192]{4,1,3,2,0:T(8,128)(2,1)S(1)} copy(bf16[2,8,36,6,192]{4,3,2,1,0:T(8,128)(2,1)S(1)} %reshape.107) | data formatting | bytes 2654208 | tf_op jit(solution)/shard_map/reshape | solution.py:72
  122.6 0.3 fusion.9
  123.1 10.3 %collective-permute-done.3 = bf16[2,8,34,1,192]{4,1,3,2,0:T(8,128)(2,1)S(1)} collective-permute-done((bf16[2,8,34,1,192]{4,1,3,2,0:T(8,128)(2,1)S(1)}, bf16[2,8,34,1,192]{4,1,3,2,0:T(8,128)(2,1)S(1)}, u32[]{:S(2)}, u32[]{:S(2)}) %collective-permute-start.3) | collective-permute-done | bytes 208928 | tf_op jit(solution)/shard_map/ppermute | solution.py:10
  133.3 1.5 %maximum_select_fusion = bf16[2,8,34,6,192]{4,1,3,2,0:T(8,128)(2,1)} fusion(bf16[2,8,34,5,192]{4,1,3,2,0:T(8,128)(2,1)S(1)} %slice.31, bf16[2,8,34,1,192]{4,1,3,2,0:T(8,128)(2,1)S(1)} %collective-permute-done.3, pred[34]{0:T(512)(128)(4,1)S(1)} %iota_compare_fusion.1), kind=kLoop, calls=%fused_computation.20 | loop fusion | flops 1253376 | bytes 2506786 | tf_op jit(solution)/shard_map/jit(_where)/select_n | solution.py:83
  (46 shorter events, 2.2 us)
Async XLA Ops:
  0.0 107.7 %copy-start = (bf16[192,192]{1,0:T(8,128)(2,1)S(1)}, bf16[192,192]{1,0:T(8,128)(2,1)}, u32[]{:S(2)}) copy-start(bf16[192,192]{1,0:T(8,128)(2,1)} %param.17) | copy-start | bytes 221188
  4.2 7.8 %copy-start.4 = (bf16[48,384]{1,0:T(8,128)(2,1)S(1)}, bf16[48,384]{1,0:T(8,128)(2,1)}, u32[]{:S(2)}) copy-start(bf16[48,384]{1,0:T(8,128)(2,1)} %param.13) | copy-start | bytes 110596
  5.0 30.0 %copy-start.5 = (bf16[24,768]{1,0:T(8,128)(2,1)S(1)}, bf16[24,768]{1,0:T(8,128)(2,1)}, u32[]{:S(2)}) copy-start(bf16[24,768]{1,0:T(8,128)(2,1)} %param.14) | copy-start | bytes 110596
  5.0 50.4 %collective-permute-start = (bf16[2,8,34,1,192]{4,1,3,2,0:T(8,128)(2,1)}, bf16[2,8,34,1,192]{4,1,3,2,0:T(8,128)(2,1)S(1)}, u32[]{:S(2)}, u32[]{:S(2)}) collective-permute-start(bf16[2,8,34,1,192]{4,1,3,2,0:T(8,128)(2,1)} %slice.29), channel_id=1, source_target_pairs={{8,0},{16,8},{24,16},{0,24},{9,1},{17,9},{25,17},{1,25},{10,2},{18... | collective-permute-start | bytes 626696 | tf_op jit(solution)/shard_map/ppermute | solution.py:10
  55.4 3.1 %collective-permute-start.1 = (bf16[2,8,1,6,192]{4,1,3,2,0:T(8,128)(2,1)S(1)}, bf16[2,8,1,6,192]{4,1,3,2,0:T(8,128)(2,1)S(1)}, u32[]{:S(2)}, u32[]{:S(2)}) collective-permute-start(bf16[2,8,1,6,192]{4,1,3,2,0:T(8,128)(2,1)S(1)} %pad_maximum_fusion), channel_id=1, source_target_pairs={{2,0},{4,2},{6,4},{3,1},{5,3},{7,5},{10,8},{12,10},{14,12},{11,9},... | collective-permute-start | bytes 110600 | tf_op jit(solution)/shard_map/ppermute | solution.py:16
  58.5 0.6 copy-start.3
  71.7 4.8 %copy-start.2 = (bf16[768,384]{1,0:T(8,128)(2,1)S(1)}, bf16[768,384]{1,0:T(8,128)(2,1)}, u32[]{:S(2)}) copy-start(bf16[768,384]{1,0:T(8,128)(2,1)} %all_gather.6) | copy-start | bytes 1769476
  71.7 4.9 %copy-start.8 = (f32[768]{0:T(1024)S(1)}, f32[768]{0:T(1024)}, u32[]{:S(2)}) copy-start(f32[768]{0:T(1024)} %param.12) | copy-start | bytes 9220
  71.7 4.9 %copy-start.9 = (f32[768]{0:T(1024)S(1)}, f32[768]{0:T(1024)}, u32[]{:S(2)}) copy-start(f32[768]{0:T(1024)} %param.11) | copy-start | bytes 9220
  92.4 5.9 %copy-start.1 = (f32[2,8,18,3,2,2,192]{6,5,4,3,2,1,0:T(2,128)S(1)}, f32[2,8,18,3,2,2,192]{6,5,4,3,2,1,0:T(2,128)}, u32[]{:S(2)}) copy-start(f32[2,8,18,3,2,2,192]{6,5,4,3,2,1,0:T(2,128)} %reshape.105) | copy-start | bytes 7962628
  106.7 1.0 copy-start.6
  106.7 1.0 copy-start.7
  116.1 6.5 %collective-permute-start.2 = (bf16[2,8,1,6,192]{4,3,2,1,0:T(8,128)(2,1)S(1)}, bf16[2,8,1,6,192]{4,3,2,1,0:T(8,128)(2,1)S(1)}, u32[]{:S(2)}, u32[]{:S(2)}) collective-permute-start(bf16[2,8,1,6,192]{4,3,2,1,0:T(8,128)(2,1)S(1)} %constant_dynamic-slice_fusion), channel_id=1, source_target_pairs={{0,2},{2,4},{4,6},{1,3},{3,5},{5,7},{8,10},{10,12},{12,14},{9,11},... | collective-permute-start | bytes 110600 | tf_op jit(solution)/shard_map/ppermute | solution.py:16
  122.9 10.4 %collective-permute-start.3 = (bf16[2,8,34,1,192]{4,1,3,2,0:T(8,128)(2,1)S(1)}, bf16[2,8,34,1,192]{4,1,3,2,0:T(8,128)(2,1)S(1)}, u32[]{:S(2)}, u32[]{:S(2)}) collective-permute-start(bf16[2,8,34,1,192]{4,1,3,2,0:T(8,128)(2,1)S(1)} %slice.30), channel_id=1, source_target_pairs={{24,0},{0,8},{8,16},{16,24},{25,1},{1,9},{9,17},{17,25},{26,2},{2,... | collective-permute-start | bytes 626696 | tf_op jit(solution)/shard_map/ppermute | solution.py:10
where the time goes:
time: 136 us; the launch traced here: 135 us
  blocking collectives  43.4 us (32%)
  local copies, waits for them, and re-layouts  38.6 us (28%)
  other arithmetic  19.2 us (14%)
  waiting for transfers between devices  11.8 us (9%)
  starting transfers between devices  11 us (8%)
  matrix products  7.64 us (6%)
  between operations  3.41 us (3%)
    all_gather x1, blocking collectives, body(): lax.all_gather(down_weight, ('lon', 'lat'), axis=0, tiled=True)  22.9 us
    all_gather x1, blocking collectives, body(): lax.all_gather(up_weight, ('lon', 'lat'), axis=0, tiled=True)  20.4 us
    convert_element_type x2, local copies, waits for them, and re-layouts, body(): merged.astype(jnp.float32)  11.4 us
    ppermute x2, waiting for transfers between devices, shifted(): return lax.ppermute(block, axis, route)  10.3 us
    reshape x2, local copies, waits for them, and re-layouts, body(): grown = grown.reshape(members, levels, half_rows, half_cols, 2, 2, features)  9.24 us
    reduce_sum x2, other arithmetic, normalize(): spread = jnp.mean(centred * centred, axis=-1, keepdims=True)  6.61 us
    ppermute x2, starting transfers between devices, passed_along(): return lax.ppermute(block, axis, route)  5.84 us
    reshape x1, local copies, waits for them, and re-layouts, body(): grown.transpose(0, 1, 2, 4, 3, 5, 6)  5.4 us
  transfers between devices with their start and end apart: 4, of which 2 were waited for; matrix products, arithmetic and copies ran while one was open for 2% of the time, Pallas kernels for 0%

commit v1 on v0

--- a/solution.py
+++ b/solution.py
@@ -51,7 +51,15 @@
     columns_used = merged_norm
     coarse = jnp.dot(
         columns_used,
-        lax.all_gather(down_weight, ("lon", "lat"), axis=0, tiled=True),
+        jnp.concatenate(
+            lax.all_to_all(
+                jnp.stack(lax.axis_size(("lon", "lat")) * [down_weight]),
+                axis_name=("lon", "lat"),
+                split_axis=0,
+                concat_axis=0,
+            ),
+            axis=0,
+        ),
         preferred_element_type=jnp.float32,
     )
     coarse = coarse.astype(jnp.bfloat16)

time: 136 us -> 109 us (0.80)
  blocking collectives: 43.4 us -> 27.2 us
  local copies, waits for them, and re-layouts: 38.6 us -> 28.3 us
  starting transfers between devices: 11 us -> 16.3 us
  other arithmetic: 19.2 us -> 15.5 us
    all_gather x1 -> x0, blocking collectives: 22.9 us -> none  [body(): lax.all_gather(down_weight, ('lon', 'lat'), axis=0, tiled=True)]
    convert_element_type x2, local copies, waits for them, and re-layouts: 11.4 us -> 3.66 us  [body(): normalize(merged.astype(jnp.float32), down_gain, down_shift)]
    all_gather x1, blocking collectives: 20.4 us -> 27.2 us  [body(): lax.all_gather(up_weight, ('lon', 'lat'), axis=0, tiled=True)]
    all_to_all x0 -> x1, starting transfers between devices: none -> 4.38 us  [body(): lax.all_to_all(jnp.stack(lax.axis_size(('lon', 'lat')) * [down_weight]),...]
    reshape x2, local copies, waits for them, and re-layouts: 9.24 us -> 7.43 us  [body(): grown = grown.reshape(members, levels, half_rows, half_cols, 2, 2, features)]
    convert_element_type x1, other arithmetic: 2.27 us -> 0.71 us  [body(): normalize(merged.astype(jnp.float32), down_gain, down_shift)]
    reduce_sum x2, other arithmetic: 6.61 us -> 5.11 us  [normalize(): spread = jnp.mean(centred * centred, axis=-1, keepdims=True)]
  transfers between devices with their start and end apart: 4 -> 5, of which waited for: 2 -> 2; matrix products, arithmetic and copies ran while one was open for 2% -> 9% of each run, Pallas kernels for 0% -> 0%
where the time goes in v1:
time: 109 us; the launch traced here: 108 us
  local copies, waits for them, and re-layouts  28.3 us (26%)
  blocking collectives  27.2 us (25%)
  starting transfers between devices  16.3 us (15%)
  other arithmetic  15.5 us (14%)
  waiting for transfers between devices  10.6 us (10%)
  matrix products  6.39 us (6%)
  between operations  3.72 us (3%)
    all_gather x1, blocking collectives, body(): lax.all_gather(up_weight, ('lon', 'lat'), axis=0, tiled=True)  27.2 us
    ppermute x2, waiting for transfers between devices, shifted(): return lax.ppermute(block, axis, route)  9.29 us
    reshape x2, local copies, waits for them, and re-layouts, body(): grown = grown.reshape(members, levels, half_rows, half_cols, 2, 2, features)  7.43 us
    ppermute x2, starting transfers between devices, shifted(): return lax.ppermute(block, axis, route)  6.13 us
    ppermute x2, starting transfers between devices, passed_along(): return lax.ppermute(block, axis, route)  5.84 us
    reshape x1, local copies, waits for them, and re-layouts, body(): grown.transpose(0, 1, 2, 4, 3, 5, 6)  5.41 us
    reduce_sum x2, other arithmetic, normalize(): spread = jnp.mean(centred * centred, axis=-1, keepdims=True)  5.11 us
    reduce_sum x2, other arithmetic, normalize(): average = jnp.mean(values, axis=-1, keepdims=True)  4.81 us
  transfers between devices with their start and end apart: 5, of which 2 were waited for; matrix products, arithmetic and copies ran while one was open for 9% of the time, Pallas kernels for 0%

profile of v1, /device:TPU:0, one launch (start us, length us, event | category | flops | bytes accessed | tf_op | source)
XLA Modules:
  0.0 108.1 jit_solution(517471424172617197)
XLA Ops:
  0.0 1.3 %fusion.19 = (s32[1,1]{1,0:T(1,128)}, s32[1,1]{1,0:T(1,128)}) fusion(s32[1,2]{1,0:T(1,128)} %param.10), kind=kLoop, calls=%fused_computation.41 | loop fusion | bytes 16 | tf_op jit(solution)/shard_map/slice | solution.py:32
  2.7 1.6 %broadcast_select_fusion = bf16[2,8,34,6,192]{4,1,3,2,0:T(8,128)(2,1)S(1)} fusion(bf16[2,8,34,6,192]{4,1,3,2,0:T(8,128)(2,1)} %param.9, pred[34]{0:T(512)(128)(4,1)S(1)} %iota_compare_fusion.1), kind=kLoop, calls=%fused_computation.26 | loop fusion | flops 626688 | bytes 2506786 | tf_op jit(solution)/shard_map/jit(_where)/select_n | solution.py:35
  4.3 0.7 slice.29
  5.0 5.1 %collective-permute-start = (bf16[2,8,34,1,192]{4,1,3,2,0:T(8,128)(2,1)}, bf16[2,8,34,1,192]{4,1,3,2,0:T(8,128)(2,1)S(1)}, u32[]{:S(2)}, u32[]{:S(2)}) collective-permute-start(bf16[2,8,34,1,192]{4,1,3,2,0:T(8,128)(2,1)} %slice.29), channel_id=1, source_target_pairs={{8,0},{16,8},{24,16},{0,24},{9,1},{17,9},{25,17},{1,25},{10,2},{18... | collective-permute-start | bytes 626696 | tf_op jit(solution)/shard_map/ppermute | solution.py:10
  10.1 0.9 stack.2
  11.0 4.4 %all-to-all-start = ((bf16[16,48,384]{2,1,0:T(8,128)(2,1)}), bf16[16,48,384]{2,1,0:T(8,128)(2,1)}, u32[]{:S(2)}, u32[]{:S(2)}) async-start(bf16[16,48,384]{2,1,0:T(8,128)(2,1)} %stack.2), calls=%async_computation | async-start | bytes 1179648 | tf_op jit(solution)/shard_map/all_to_all | solution.py:55
  17.6 27.2 %all_gather.3 = bf16[384,768]{1,0:T(8,128)(2,1)} all-gather(bf16[24,768]{1,0:T(8,128)(2,1)S(1)} %copy-done.4), channel_id=1, replica_groups=mesh['lon'=4,'lat'=4,'mem'=2] {'lon','lat'}, dimensions={0}, use_global_device_ids=true | all-gather | bytes 626688 | tf_op jit(solution)/shard_map/all_gather | solution.py:69
  44.9 1.3 %collective-permute-start.1 = (bf16[2,8,1,6,192]{4,1,3,2,0:T(8,128)(2,1)S(1)}, bf16[2,8,1,6,192]{4,1,3,2,0:T(8,128)(2,1)S(1)}, u32[]{:S(2)}, u32[]{:S(2)}) collective-permute-start(bf16[2,8,1,6,192]{4,1,3,2,0:T(8,128)(2,1)S(1)} %pad_maximum_fusion), channel_id=1, source_target_pairs={{2,0},{4,2},{6,4},{3,1},{5,3},{7,5},{10,8},{12,10},{14,12},{11,9},... | collective-permute-start | bytes 110600 | tf_op jit(solution)/shard_map/ppermute | solution.py:16
  46.7 1.3 %collective-permute-done.1 = bf16[2,8,1,6,192]{4,1,3,2,0:T(8,128)(2,1)S(1)} collective-permute-done((bf16[2,8,1,6,192]{4,1,3,2,0:T(8,128)(2,1)S(1)}, bf16[2,8,1,6,192]{4,1,3,2,0:T(8,128)(2,1)S(1)}, u32[]{:S(2)}, u32[]{:S(2)}) %collective-permute-start.1) | collective-permute-done | bytes 36896 | tf_op jit(solution)/shard_map/ppermute | solution.py:16
  48.0 0.6 fusion.11
  48.6 0.4 fusion.1
  49.0 0.7 fusion.4
  49.8 0.7 fusion.7
  50.5 1.4 %copy.21 = bf16[2,8,18,3,2,2,192]{6,5,4,3,2,1,0:T(2,128)(2,1)S(1)} copy(bf16[2,8,18,3,2,2,192]{6,1,4,3,5,2,0:T(8,128)(2,1)S(1)} %fusion.7) | data formatting | bytes 2654208 | tf_op jit(solution)/shard_map/convert_element_type | solution.py:50
  51.9 2.3 %convert_element_type.32 = bf16[864,768]{1,0:T(8,128)(2,1)} reshape(bf16[2,8,18,3,2,2,192]{6,5,4,3,2,1,0:T(2,128)(2,1)S(1)} %copy.21) | data formatting | bytes 2654208 | tf_op jit(solution)/shard_map/convert_element_type | solution.py:50
  54.2 3.1 %fusion.17 = f32[864,768]{1,0:T(8,128)S(1)} fusion(bf16[384,768]{1,0:T(8,128)(2,1)S(1)} %copy-done.2, bf16[864,768]{1,0:T(8,128)(2,1)} %convert_element_type.32, bf16[768,384]{1,0:T(8,128)(2,1)} %bitcast.6), kind=kOutput, calls=%fused_computation.28 | convolution fusion | flops 1019547648 | bytes 5160960 | tf_op jit(solution)/shard_map/dot_general | solution.py:67
  57.3 4.5 %reshape.119 = f32[2,8,18,3,2,2,192]{6,5,4,3,2,1,0:T(2,128)} reshape(f32[864,768]{1,0:T(8,128)S(1)} %fusion.17) | data formatting | bytes 5308416 | tf_op jit(solution)/shard_map/reshape | solution.py:72
  61.8 4.4 %fusion.18 = f32[2,8,18,2,3,2]{5,4,3,2,1,0:T(4,128)S(1)} fusion(f32[2,8,18,3,2,2,192]{6,5,4,3,2,1,0:T(2,128)} %reshape.119), kind=kLoop, calls=%fused_computation.40 | loop fusion | flops 660096 | bytes 2668032 | tf_op jit(solution)/shard_map/reduce_sum | solution.py:20
  66.2 3.0 %copy.32 = f32[2,8,18,3,2,2,192]{6,5,3,4,2,1,0:T(2,128)} copy(f32[2,8,18,3,2,2,192]{6,5,4,3,2,1,0:T(2,128)S(1)} %copy-done.1) | data formatting | bytes 5308416 | tf_op jit(solution)/shard_map/reshape | solution.py:72
  69.5 4.4 %multiply_reduce_fusion = f32[2,8,18,2,3,2]{5,4,3,2,1,0:T(4,128)S(1)} fusion(f32[2,8,18,2,3,2]{5,4,3,2,1,0:T(4,128)S(1)} %broadcast_multiply_fusion, f32[2,8,18,3,2,2,192]{6,5,4,3,2,1,0:T(2,128)S(1)} %copy-done.1), kind=kLoop, calls=%fused_computation.12 | loop fusion | flops 1987200 | bytes 2681856 | tf_op jit(solution)/shard_map/reduce_sum | solution.py:22
  73.9 0.6 div.17
  74.5 0.4 add_rsqrt_fusion
  74.9 0.6 rsqrt.21
  75.5 5.4 %reshape.120 = f32[3456,192]{1,0:T(8,128)} reshape(f32[2,8,18,2,3,2,192]{6,5,4,3,2,1,0:T(2,128)} %bitcast.42) | data formatting | bytes 5308416 | tf_op jit(solution)/shard_map/reshape | solution.py:73
  80.9 3.3 %convolution_convert_fusion = bf16[3456,192]{0,1:T(8,128)(2,1)S(1)} fusion(bf16[192,192]{1,0:T(8,128)(2,1)S(1)} %copy-done, f32[3456,192]{1,0:T(8,128)} %reshape.120, f32[192]{0:T(256)S(1)} %copy-done.7, f32[192]{0:T(256)S(1)} %copy-done.8, f32[3456]{0:T(1024)S(1)} %rsqrt.21, f32[3456]{0:T(1024)S(1)} %div.17), kind=kOutput, calls=%fused_computation | convolution fusion | flops 258785280 | bytes 4084224 | tf_op jit(solution)/shard_map/dot_general | solution.py:77
  84.2 2.3 %copy.23 = bf16[3456,192]{1,0:T(8,128)(2,1)} copy(bf16[3456,192]{0,1:T(8,128)(2,1)S(1)} %convolution_convert_fusion) | data formatting | bytes 2654208 | tf_op jit(solution)/shard_map/convert_element_type | solution.py:80
  86.5 2.8 %reshape.121 = bf16[2,8,36,6,192]{4,3,2,1,0:T(8,128)(2,1)S(1)} reshape(bf16[3456,192]{1,0:T(8,128)(2,1)} %copy.23) | data formatting | bytes 2654208 | tf_op jit(solution)/shard_map/reshape | solution.py:80
  89.3 4.5 %collective-permute-start.2 = (bf16[2,8,1,6,192]{4,3,2,1,0:T(8,128)(2,1)S(1)}, bf16[2,8,1,6,192]{4,3,2,1,0:T(8,128)(2,1)S(1)}, u32[]{:S(2)}, u32[]{:S(2)}) collective-permute-start(bf16[2,8,1,6,192]{4,3,2,1,0:T(8,128)(2,1)S(1)} %constant_dynamic-slice_fusion), channel_id=1, source_target_pairs={{0,2},{2,4},{4,6},{1,3},{3,5},{5,7},{8,10},{10,12},{12,14},{9,11},... | collective-permute-start | bytes 110600 | tf_op jit(solution)/shard_map/ppermute | solution.py:16
  93.9 1.9 %copy.25 = bf16[2,8,36,6,192]{4,1,3,2,0:T(8,128)(2,1)S(1)} copy(bf16[2,8,36,6,192]{4,3,2,1,0:T(8,128)(2,1)S(1)} %reshape.121) | data formatting | bytes 2654208 | tf_op jit(solution)/shard_map/reshape | solution.py:80
  96.2 1.0 collective-permute-start.3
  97.3 9.3 %collective-permute-done.3 = bf16[2,8,34,1,192]{4,1,3,2,0:T(8,128)(2,1)S(1)} collective-permute-done((bf16[2,8,34,1,192]{4,1,3,2,0:T(8,128)(2,1)S(1)}, bf16[2,8,34,1,192]{4,1,3,2,0:T(8,128)(2,1)S(1)}, u32[]{:S(2)}, u32[]{:S(2)}) %collective-permute-start.3) | collective-permute-done | bytes 208928 | tf_op jit(solution)/shard_map/ppermute | solution.py:10
  106.6 1.5 %maximum_select_fusion = bf16[2,8,34,6,192]{4,1,3,2,0:T(8,128)(2,1)} fusion(bf16[2,8,34,5,192]{4,1,3,2,0:T(8,128)(2,1)S(1)} %slice.31, bf16[2,8,34,1,192]{4,1,3,2,0:T(8,128)(2,1)S(1)} %collective-permute-done.3, pred[34]{0:T(512)(128)(4,1)S(1)} %iota_compare_fusion.1), kind=kLoop, calls=%fused_computation.25 | loop fusion | flops 1253376 | bytes 2506786 | tf_op jit(solution)/shard_map/jit(_where)/select_n | solution.py:91
  (43 shorter events, 1.5 us)
Async XLA Ops:
  0.0 80.9 %copy-start = (bf16[192,192]{1,0:T(8,128)(2,1)S(1)}, bf16[192,192]{1,0:T(8,128)(2,1)}, u32[]{:S(2)}) copy-start(bf16[192,192]{1,0:T(8,128)(2,1)} %param.17) | copy-start | bytes 221188
  2.7 7.5 %copy-start.3 = (bf16[48,384]{1,0:T(8,128)(2,1)S(1)}, bf16[48,384]{1,0:T(8,128)(2,1)}, u32[]{:S(2)}) copy-start(bf16[48,384]{1,0:T(8,128)(2,1)} %param.13) | copy-start | bytes 110596
  5.0 39.8 %collective-permute-start = (bf16[2,8,34,1,192]{4,1,3,2,0:T(8,128)(2,1)}, bf16[2,8,34,1,192]{4,1,3,2,0:T(8,128)(2,1)S(1)}, u32[]{:S(2)}, u32[]{:S(2)}) collective-permute-start(bf16[2,8,34,1,192]{4,1,3,2,0:T(8,128)(2,1)} %slice.29), channel_id=1, source_target_pairs={{8,0},{16,8},{24,16},{0,24},{9,1},{17,9},{25,17},{1,25},{10,2},{18... | collective-permute-start | bytes 626696 | tf_op jit(solution)/shard_map/ppermute | solution.py:10
  11.0 6.6 %copy-start.4 = (bf16[24,768]{1,0:T(8,128)(2,1)S(1)}, bf16[24,768]{1,0:T(8,128)(2,1)}, u32[]{:S(2)}) copy-start(bf16[24,768]{1,0:T(8,128)(2,1)} %param.14) | copy-start | bytes 110596
  11.0 43.2 %all-to-all-start = ((bf16[16,48,384]{2,1,0:T(8,128)(2,1)}), bf16[16,48,384]{2,1,0:T(8,128)(2,1)}, u32[]{:S(2)}, u32[]{:S(2)}) async-start(bf16[16,48,384]{2,1,0:T(8,128)(2,1)} %stack.2), calls=%async_computation | async-start | bytes 1179648 | tf_op jit(solution)/shard_map/all_to_all | solution.py:55
  17.6 28.9 %copy-start.5 = (f32[768]{0:T(1024)S(1)}, f32[768]{0:T(1024)}, u32[]{:S(2)}) copy-start(f32[768]{0:T(1024)} %param.11) | copy-start | bytes 9220
  17.6 29.0 %copy-start.6 = (f32[768]{0:T(1024)S(1)}, f32[768]{0:T(1024)}, u32[]{:S(2)}) copy-start(f32[768]{0:T(1024)} %param.12) | copy-start | bytes 9220
  44.9 3.1 %collective-permute-start.1 = (bf16[2,8,1,6,192]{4,1,3,2,0:T(8,128)(2,1)S(1)}, bf16[2,8,1,6,192]{4,1,3,2,0:T(8,128)(2,1)S(1)}, u32[]{:S(2)}, u32[]{:S(2)}) collective-permute-start(bf16[2,8,1,6,192]{4,1,3,2,0:T(8,128)(2,1)S(1)} %pad_maximum_fusion), channel_id=1, source_target_pairs={{2,0},{4,2},{6,4},{3,1},{5,3},{7,5},{10,8},{12,10},{14,12},{11,9},... | collective-permute-start | bytes 110600 | tf_op jit(solution)/shard_map/ppermute | solution.py:16
  51.9 2.3 %copy-start.2 = (bf16[384,768]{1,0:T(8,128)(2,1)S(1)}, bf16[384,768]{1,0:T(8,128)(2,1)}, u32[]{:S(2)}) copy-start(bf16[384,768]{1,0:T(8,128)(2,1)} %all_gather.3) | copy-start | bytes 1769476
  61.8 4.4 %copy-start.1 = (f32[2,8,18,3,2,2,192]{6,5,4,3,2,1,0:T(2,128)S(1)}, f32[2,8,18,3,2,2,192]{6,5,4,3,2,1,0:T(2,128)}, u32[]{:S(2)}) copy-start(f32[2,8,18,3,2,2,192]{6,5,4,3,2,1,0:T(2,128)} %reshape.119) | copy-start | bytes 7962628
  75.5 5.4 %copy-start.7 = (f32[192]{0:T(256)S(1)}, f32[192]{0:T(256)}, u32[]{:S(2)}) copy-start(f32[192]{0:T(256)} %param.16) | copy-start | bytes 2308
  75.5 5.4 %copy-start.8 = (f32[192]{0:T(256)S(1)}, f32[192]{0:T(256)}, u32[]{:S(2)}) copy-start(f32[192]{0:T(256)} %param.15) | copy-start | bytes 2308
  89.3 6.5 %collective-permute-start.2 = (bf16[2,8,1,6,192]{4,3,2,1,0:T(8,128)(2,1)S(1)}, bf16[2,8,1,6,192]{4,3,2,1,0:T(8,128)(2,1)S(1)}, u32[]{:S(2)}, u32[]{:S(2)}) collective-permute-start(bf16[2,8,1,6,192]{4,3,2,1,0:T(8,128)(2,1)S(1)} %constant_dynamic-slice_fusion), channel_id=1, source_target_pairs={{0,2},{2,4},{4,6},{1,3},{3,5},{5,7},{8,10},{10,12},{12,14},{9,11},... | collective-permute-start | bytes 110600 | tf_op jit(solution)/shard_map/ppermute | solution.py:16
  96.2 10.4 %collective-permute-start.3 = (bf16[2,8,34,1,192]{4,1,3,2,0:T(8,128)(2,1)S(1)}, bf16[2,8,34,1,192]{4,1,3,2,0:T(8,128)(2,1)S(1)}, u32[]{:S(2)}, u32[]{:S(2)}) collective-permute-start(bf16[2,8,34,1,192]{4,1,3,2,0:T(8,128)(2,1)S(1)} %slice.30), channel_id=1, source_target_pairs={{24,0},{0,8},{8,16},{16,24},{25,1},{1,9},{9,17},{17,25},{26,2},{2,... | collective-permute-start | bytes 626696 | tf_op jit(solution)/shard_map/ppermute | solution.py:10
